TPU v7x, 32 devices: a whole 2x2x4 slice. The times are simulated.
32 devices in a mesh: inst: 4 (over x, core), dp: 4 (over z), tp: 2 (over y).
Axes of the slice: x: 2, y: 2, z: 4, core: 2. Of those that a mesh axis runs over, the one named last changes fastest.
Arguments:
- kernel_grads: bfloat16 [16, 2, 128, 4608], P(('inst', 'dp'), 'tp'), may hold values from -0.75 to 0.75
- kernel_master: float32 [2, 128, 4608], P('tp', 'dp'), may hold values from -6 to 6
- kernel_first: float32 [2, 128, 4608], P('tp', 'dp'), may hold values from -3 to 3
- kernel_second: float32 [2, 128, 4608], P('tp', 'dp'), may hold values from 0.05 to 4
- gain_grads: bfloat16 [32, 4, 4608], P(('inst', 'dp', 'tp')), may hold values from -0.29882812 to 0.29882812
- gain_master: float32 [4, 4608], replicated, may hold values from -6 to 6
- gain_first: float32 [4, 4608], replicated, may hold values from -3 to 3
- gain_second: float32 [4, 4608], replicated, may hold values from 0.05 to 4
Outputs:
- kernel_params: bfloat16 [2, 128, 4608], P('tp')
- kernel_master_new: float32 [2, 128, 4608], P('tp', 'dp')
- kernel_first_new: float32 [2, 128, 4608], P('tp', 'dp')
- kernel_second_new: float32 [2, 128, 4608], P('tp', 'dp')
- gain_params: bfloat16 [4, 4608], replicated
- gain_master_new: float32 [4, 4608], replicated
- gain_first_new: float32 [4, 4608], replicated
- gain_second_new: float32 [4, 4608], replicated
All inputs are finite; a program needn't handle non-finite values.
Results may differ from a plain program's by a relative error of at most 0.004.
Values may be sent and summed in bfloat16 or wider, within the bound.
A program may use at most 64 MiB of HBM per device.

v0:
```python
import jax
import jax.numpy as jnp
from jax import lax
from jax.sharding import PartitionSpec as P

beta_one = 0.9
beta_two = 0.95
learn_rate = 0.01
decay_rate = 0.1
epsilon = 1e-08
step_count = 100.0


def adam_update(gradient, master, first_moment, second_moment):
    first_next = beta_one * first_moment + (1.0 - beta_one) * gradient
    second_next = beta_two * second_moment + (1.0 - beta_two) * gradient * gradient
    first_hat = first_next / (1.0 - beta_one**step_count)
    second_hat = second_next / (1.0 - beta_two**step_count)
    master_next = master - learn_rate * (
        first_hat / (jnp.sqrt(second_hat) + epsilon) + decay_rate * master
    )
    return (master_next, first_next, second_next)


def local(
    kernel_grads,
    kernel_master,
    kernel_first,
    kernel_second,
    gain_grads,
    gain_master,
    gain_first,
    gain_second,
):
    local_grads = kernel_grads[0].astype(jnp.float32)
    gain_local = gain_grads[0].astype(jnp.float32)
    flat_grads = gain_local.reshape(-1)
    gain_whole = None
    partial_rows, gain_piece = (
        lax.psum_scatter(
            local_grads.astype(jnp.bfloat16), "dp", scatter_dimension=1, tiled=True
        ).astype(jnp.float32),
        lax.psum_scatter(
            flat_grads.astype(jnp.bfloat16), "dp", scatter_dimension=0, tiled=True
        ).astype(jnp.float32),
    )
    gradient, gain_piece = (
        lax.psum(partial_rows.astype(jnp.bfloat16), "inst").astype(jnp.float32),
        lax.psum(gain_piece.astype(jnp.bfloat16), "inst").astype(jnp.float32),
    )
    kernel_master_new, kernel_first_new, kernel_second_new = adam_update(
        gradient, kernel_master, kernel_first, kernel_second
    )
    kernel_params = lax.all_gather(kernel_master_new.astype(jnp.bfloat16), "dp", axis=1, tiled=True)
    gain_piece = lax.psum(gain_piece, "tp")
    gain_whole = lax.all_gather(gain_piece, "dp", axis=0, tiled=True).reshape(gain_master.shape)
    gain_master_new, gain_first_new, gain_second_new = adam_update(
        gain_whole, gain_master, gain_first, gain_second
    )
    gain_params = gain_master_new.astype(jnp.bfloat16)
    return (
        kernel_params,
        kernel_master_new,
        kernel_first_new,
        kernel_second_new,
        gain_params,
        gain_master_new,
        gain_first_new,
        gain_second_new,
    )


def solution(mesh):
    return jax.shard_map(
        local,
        mesh=mesh,
        in_specs=(
            P(("inst", "dp"), "tp", None, None),
            P("tp", "dp", None),
            P("tp", "dp", None),
            P("tp", "dp", None),
            P(("inst", "dp", "tp"), None, None),
            P(),
            P(),
            P(),
        ),
        out_specs=(
            P("tp", None, None),
            P("tp", "dp", None),
            P("tp", "dp", None),
            P("tp", "dp", None),
            P(),
            P(),
            P(),
            P(),
        ),
        check_vma=False,
    )
```

profile of v0, /device:TPU:0, one launch (start us, length us, event | category | flops | bytes accessed | tf_op | source)
XLA Modules:
  0.0 142.5 jit_solution(16182226304347898728)
XLA Ops:
  7.2 0.0 copy-start.1
  7.2 0.0 copy-start
  7.2 0.0 reduce-scatter.2.cloned.1.call-start
  7.2 0.7 reduce-scatter.2.cloned.1.call-update
  7.9 0.0 all-reduce.3.cloned.1.call-start
  8.0 34.4 %reduce-scatter.2.cloned.1.call-done = bf16[1,32,4608]{2,1,0:T(8,128)(2,1)} async-done(((bf16[1,128,4608]{2,1,0:T(8,128)(2,1)}), bf16[1,32,4608]{2,1,0:T(8,128)(2,1)}) %reduce-scatter.2.cloned.1.call-update) | async-done | bytes 294928 | tf_op jit(solution)/shard_map/reduce_scatter | solution.py:40
  42.4 0.0 all-reduce.3.cloned.1.call-update
  42.4 0.0 copy-start.5
  42.4 0.0 copy-start.6
  42.4 0.0 copy-start.2
  42.4 0.0 copy-start.3
  42.5 0.0 copy-start.4
  42.5 0.0 all-gather.3.cloned.1.call-start
  42.5 33.3 %all-reduce.3.cloned.1.call-done = bf16[1,32,4608]{2,1,0:T(8,128)(2,1)} async-done(((bf16[1,32,4608]{2,1,0:T(8,128)(2,1)}), bf16[1,32,4608]{2,1,0:T(8,128)(2,1)}) %all-reduce.3.cloned.1.call-update) | async-done | bytes 294928 | tf_op jit(solution)/shard_map/psum | solution.py:48
  75.8 0.0 copy-done.1
  75.8 0.0 copy-done
  75.8 2.7 %fusion.7 = (bf16[1,32,4608]{2,1,0:T(8,128)(2,1)}, f32[1,32,4608]{2,1,0:T(8,128)}, f32[1,32,4608]{2,1,0:T(8,128)}, f32[1,32,4608]{2,1,0:T(8,128)}) fusion(f32[1,32,4608]{2,1,0:T(8,128)S(1)} %copy-done, bf16[1,32,4608]{2,1,0:T(8,128)(2,1)} %all-reduce.3.cloned.1.call-done, f32[1,32,4608]{2,1,0:T(8,128)S(1)} %copy-done.1, f32[1,32,4608]{2,1,0:T(8,128)} %param.11), kind=kLoop, calls=%fused_computation.11 | loop fusion | flops 2506752 | bytes 4128768 | tf_op jit(solution)/shard_map/convert_element_type | solution.py:54
  78.5 0.0 all-gather.3.cloned.1.call-update
  78.6 0.0 copy-done.5
  78.6 0.0 copy-done.6
  78.6 0.6 dynamic-slice
  79.9 20.5 %all-reduce = bf16[18432]{0:T(1024)(128)(2,1)S(1)} all-reduce(bf16[18432]{0:T(1024)(128)(2,1)S(1)} %squeeze.7), channel_id=3, replica_groups=mesh['inst'=4,'dp'=4,'tp'=2] {'dp'}, use_global_device_ids=true, to_apply=%region_2.0.clone | all-reduce | flops 18432 | bytes 73728
  100.4 0.1 dynamic-slice.1
  100.5 10.9 %psum.22 = bf16[4608]{0:T(1024)(128)(2,1)S(1)} all-reduce(bf16[4608]{0:T(1024)(128)(2,1)S(1)} %dynamic-slice.1), channel_id=1, replica_groups=mesh['inst'=4,'dp'=4,'tp'=2] {'inst'}, use_global_device_ids=true, to_apply=%region_3.0 | all-reduce | flops 4608 | bytes 18432 | tf_op jit(solution)/shard_map/psum | solution.py:49
  111.4 8.2 %psum.23 = f32[4608]{0:T(1024)S(1)} all-reduce(bf16[4608]{0:T(1024)(128)(2,1)S(1)} %psum.22), channel_id=1, replica_groups=mesh['inst'=4,'dp'=4,'tp'=2] {'tp'}, use_global_device_ids=true, to_apply=%region_4.0 | all-reduce | flops 4608 | bytes 27648 | tf_op jit(solution)/shard_map/psum | solution.py:55
  119.6 13.2 %all-gather = f32[4,1,4608]{2,1,0:T(1,128)S(1)} all-gather(f32[1,1,4608]{2,1,0:T(1,128)S(1)} %reshape.22), channel_id=1, replica_groups=mesh['inst'=4,'dp'=4,'tp'=2] {'dp'}, dimensions={0}, use_global_device_ids=true | all-gather | bytes 92160 | tf_op jit(solution)/shard_map/all_gather | solution.py:56
  132.8 0.0 copy-done.2
  132.8 0.0 copy-done.3
  132.8 0.0 copy-done.4
  132.8 0.8 fusion.4
  133.6 0.0 all-gather.3.cloned.1.call-done
  133.6 2.4 %copy.23 = bf16[1,128,4608]{2,1,0:T(8,128)(2,1)} copy(bf16[1,128,4608]{2,1,0:T(8,128)(2,1)} %all-gather.3.cloned.1.call-done) | data formatting | bytes 2359296
  (2 shorter events, 0.0 us)
Async XLA Ops:
  7.2 68.6 %copy-start.1 = (f32[1,32,4608]{2,1,0:T(8,128)S(1)}, f32[1,32,4608]{2,1,0:T(8,128)}, u32[]{:S(2)}) copy-start(f32[1,32,4608]{2,1,0:T(8,128)} %param.10) | copy-start | bytes 1769476
  7.2 68.6 %copy-start = (f32[1,32,4608]{2,1,0:T(8,128)S(1)}, f32[1,32,4608]{2,1,0:T(8,128)}, u32[]{:S(2)}) copy-start(f32[1,32,4608]{2,1,0:T(8,128)} %param.9) | copy-start | bytes 1769476
  7.2 35.2 %reduce-scatter.2.cloned.1.call-start = ((), (), s32[]{:S(2)}) async-start(), calls=%async_computation.1 | async-start | bytes 1474560 | tf_op jit(solution)/shard_map/reduce_scatter | solution.py:40
  7.9 67.9 %all-reduce.3.cloned.1.call-start = ((), (), s32[]{:S(2)}) async-start(), calls=%async_computation.2 | async-start | bytes 589824 | tf_op jit(solution)/shard_map/psum | solution.py:48
  42.4 36.2 %copy-start.5 = (bf16[1,4,4608]{2,1,0:T(4,128)(2,1)S(1)}, bf16[1,4,4608]{2,1,0:T(4,128)(2,1)}, u32[]{:S(2)}) copy-start(bf16[1,4,4608]{2,1,0:T(4,128)(2,1)} %param.12) | copy-start | bytes 110596
  42.4 36.2 %copy-start.6 = (u32[32]{0:T(128)S(1)}, u32[32]{0:T(128)}, u32[]{:S(2)}) copy-start(u32[32]{0:T(128)} %constant.35) | copy-start | bytes 388
  42.4 90.3 %copy-start.2 = (f32[4,4608]{1,0:T(4,128)S(1)}, f32[4,4608]{1,0:T(4,128)}, u32[]{:S(2)}) copy-start(f32[4,4608]{1,0:T(4,128)} %param.13) | copy-start | bytes 221188
  42.4 90.3 %copy-start.3 = (f32[4,4608]{1,0:T(4,128)S(1)}, f32[4,4608]{1,0:T(4,128)}, u32[]{:S(2)}) copy-start(f32[4,4608]{1,0:T(4,128)} %param.14) | copy-start | bytes 221188
  42.5 90.3 %copy-start.4 = (f32[4,4608]{1,0:T(4,128)S(1)}, f32[4,4608]{1,0:T(4,128)}, u32[]{:S(2)}) copy-start(f32[4,4608]{1,0:T(4,128)} %param.15) | copy-start | bytes 221188
  42.5 91.1 %all-gather.3.cloned.1.call-start = ((), (), s32[]{:S(2)}) async-start(), calls=%async_computation.3 | async-start | bytes 1474560 | tf_op jit(solution)/shard_map/all_gather | solution.py:54
Sparse Core Ops, SparseCore 0:
  10.3 32.0 reduce-scatter.1
  44.7 31.0 all-reduce.2
  78.7 30.9 all-gather.2
where the time goes:
time: 143 us; the launch traced here: 142 us
  waiting for transfers between devices  68.4 us (48%)
  blocking collectives  52.8 us (37%)
  between operations  14.5 us (10%)
  other arithmetic  3.55 us (2%)
  local copies, waits for them, and re-layouts  3.1 us (2%)
    reduce_scatter x1, waiting for transfers between devices, local(): lax.psum_scatter(local_grads.astype(jnp.bfloat16), 'dp', scatter_dimensio...  34.4 us
    psum x1, waiting for transfers between devices, local(): lax.psum(partial_rows.astype(jnp.bfloat16), 'inst').astype(jnp.float32)  33.3 us
    unnamed x1, blocking collectives  20.5 us
    all_gather x1, blocking collectives, local(): lax.all_gather(gain_piece, 'dp', axis=0, tiled=True)  13.2 us
    psum x1, blocking collectives, local(): lax.psum(gain_piece.astype(jnp.bfloat16), 'inst').astype(jnp.float32)  10.9 us
    psum x1, blocking collectives, local(): gain_piece = lax.psum(gain_piece, 'tp')  8.21 us
    unnamed x18, local copies, waits for them, and re-layouts  3.08 us
  transfers between devices with their start and end apart: 3, of which 2 were waited for; matrix products, arithmetic and copies ran while one was open for 1% of the time, Pallas kernels for 0%

commit v1 on v0

v1 whole, which is shorter than its diff:
```python
import functools

import jax
import jax.numpy as jnp
from jax import lax
from jax.experimental import pallas as pl
from jax.experimental.pallas import tpu as pltpu
from jax.sharding import PartitionSpec as P

beta_one = 0.9
beta_two = 0.95
learn_rate = 0.01
decay_rate = 0.1
epsilon = 1e-08
step_count = 100.0
MESH = pl.DeviceIdType.MESH
F32 = jnp.float32
BF16 = jnp.bfloat16


def adam_update(gradient, master, first_moment, second_moment):
    first_next = beta_one * first_moment + (1.0 - beta_one) * gradient
    second_next = beta_two * second_moment + (1.0 - beta_two) * gradient * gradient
    first_hat = first_next / (1.0 - beta_one**step_count)
    second_hat = second_next / (1.0 - beta_two**step_count)
    master_next = master - learn_rate * (
        first_hat / (jnp.sqrt(second_hat) + epsilon) + decay_rate * master
    )
    return (master_next, first_next, second_next)


def step_kernel(
    n, tp, grads, master, first, second, gains,
    params, gsum, gain_sum,
    gv, core_in, x_out, x_in, z_out, z_in, pv, mv, vv,
    nv, nc_in, nx_out, nx_in, ny, nz,
    load_sem, core_s, core_r, x_s, x_r, z_s, z_r,
    pz_s, pz_r, px_s, px_r, pc_s, pc_r, g_s, g_r,
    nc_s, nc_r, nx_s, nx_r, ny_s, ny_r, nz_s, nz_r, nf_s, nf_r,
):
    cols = gv.shape[2]
    half, quarter = cols // 2, cols // 4
    me = lax.axis_index("inst")
    z = lax.axis_index("dp")
    y = lax.axis_index("tp")
    core, x = me % 2, me // 2
    partner = me + 1 - 2 * core
    across = (me + 2) % 4
    diagonal = (partner + 2) % 4
    order = sorted(range(1, n), key=lambda j: -min(j, n - j)) + [0]
    near = sorted(range(1, n), key=lambda j: min(j, n - j))

    def span(start, size):
        return pl.ds(pl.multiple_of(start, 128), size)

    def cols_of(inst):
        return span((inst % 2) * half + (inst // 2) * quarter, quarter)

    def send(src, dst, s, r, **where):
        copy = pltpu.make_async_remote_copy(
            src_ref=src, dst_ref=dst, send_sem=s, recv_sem=r,
            device_id=where, device_id_type=MESH,
        )
        copy.start()
        return copy

    def load(src, dst, k):
        copy = pltpu.make_async_copy(src, dst, load_sem.at[k])
        copy.start()
        return copy

    to = {j: (z + j) % n for j in range(n)}
    frm = {j: (z + n - j) % n for j in range(n)}
    loads = {j: load(grads.at[to[j]], gv.at[to[j]], j) for j in order}
    load_gain = load(gains, nv, n)
    load_state = [
        load(a, b, n + 1 + k)
        for k, (a, b) in enumerate(((master, pv), (first, mv), (second, vv)))
    ]

    barrier = pltpu.get_barrier_semaphore()
    for other in (partner, across, diagonal):
        pl.semaphore_signal(barrier, inc=1, device_id={"inst": other}, device_id_type=MESH)
    for j in range(1, n):
        pl.semaphore_signal(barrier, inc=1, device_id={"dp": to[j]}, device_id_type=MESH)
    for j in range(1, tp):
        pl.semaphore_signal(
            barrier, inc=1, device_id={"tp": (y + j) % tp}, device_id_type=MESH
        )
    pl.semaphore_wait(barrier, 3 + n - 1 + tp - 1)

    mine_half, other_half = span(core * half, half), span((1 - core) * half, half)
    mine, theirs = cols_of(me), cols_of(across)
    mine_in, theirs_in = span(x * quarter, quarter), span((1 - x) * quarter, quarter)
    sent = []

    core_c = {}
    for j in order:
        loads[j].wait()
        core_c[j] = send(
            gv.at[to[j], :, other_half], core_in.at[to[j]], core_s.at[j], core_r.at[j],
            inst=partner,
        )
    load_gain.wait()
    nc = send(nv.at[:, other_half], nc_in, nc_s.at[0], nc_r.at[0], inst=partner)

    x_c = {}
    for j in order:
        core_c[j].wait_recv()
        k = to[j]
        x_out[k] = (
            gv[k, :, theirs].astype(F32) + core_in[k, :, theirs_in].astype(F32)
        ).astype(BF16)
        x_c[j] = send(x_out.at[k], x_in.at[k], x_s.at[j], x_r.at[j], inst=across)
        if j == order[0]:
            nc.wait_recv()
            nx_out[...] = (
                nv[:, theirs].astype(F32) + nc_in[:, theirs_in].astype(F32)
            ).astype(BF16)
            nx = send(nx_out, nx_in, nx_s.at[0], nx_r.at[0], inst=across)

    def chip_sum(k):
        return (
            gv[k, :, mine].astype(F32)
            + core_in[k, :, mine_in].astype(F32)
            + x_in[k].astype(F32)
        )

    z_c = {}
    ny_c, nz_c = [], []
    for j in order[:-1]:
        x_c[j].wait_recv()
        k = to[j]
        z_out[j] = chip_sum(k).astype(BF16)
        z_c[j] = send(z_out.at[j], z_in.at[j], z_s.at[j], z_r.at[j], dp=k)
        if j == order[0]:
            nx.wait_recv()
            ny[y] = (
                nv[:, mine].astype(F32) + nc_in[:, mine_in].astype(F32)
                + nx_in[...].astype(F32)
            ).astype(BF16)
            for i in range(1, tp):
                ny_c.append(
                    send(ny.at[y], ny.at[y], ny_s.at[i], ny_r.at[i], tp=(y + i) % tp)
                )
    for copy in ny_c:
        copy.wait_recv()
    total = ny[0].astype(F32)
    for i in range(1, tp):
        total += ny[i].astype(F32)
    nz[z] = total.astype(BF16)
    for j in range(1, n):
        nz_c.append(send(nz.at[z], nz.at[z], nz_s.at[j], nz_r.at[j], dp=to[j]))

    x_c[0].wait_recv()
    gradient = chip_sum(z)
    for copy in load_state:
        copy.wait()
    for j in order[:-1]:
        z_c[j].wait_recv()
        gradient += z_in[j].astype(F32)
    gsum[:, mine] = gradient.astype(BF16)

    def new_params(where):
        g = gsum[:, where].astype(F32)
        fresh = adam_update(g, pv[:, where], mv[:, where], vv[:, where])[0]
        params[z, :, where] = fresh.astype(BF16)

    new_params(mine)
    pz_c = {}
    for j in near[::-1]:
        pz_c[j] = send(
            params.at[z, :, mine], params.at[z, :, mine], pz_s.at[j], pz_r.at[j], dp=to[j]
        )
    g_x = send(gsum.at[:, mine], gsum.at[:, mine], g_s.at[0], g_r.at[0], inst=across)
    g_c = send(gsum.at[:, mine], gsum.at[:, mine], g_s.at[1], g_r.at[1], inst=partner)

    for copy in nz_c:
        copy.wait_recv()
    total = nz[0].astype(F32)
    for j in range(1, n):
        total += nz[j].astype(F32)
    gain_sum[:, mine] = total
    nf_c = [
        send(gain_sum.at[:, mine], gain_sum.at[:, mine], nf_s.at[i], nf_r.at[i], inst=other)
        for i, other in enumerate((partner, across, diagonal))
    ]

    g_x.wait_recv()
    g_f = send(gsum.at[:, theirs], gsum.at[:, theirs], g_s.at[2], g_r.at[2], inst=partner)
    px_c, pc_c, pd_c = {}, {}, {}

    def relay(j):
        pz_c[j].wait_recv()
        piece = params.at[frm[j], :, mine]
        px_c[j] = send(piece, piece, px_s.at[j], px_r.at[j], inst=across)
        pc_c[j] = send(piece, piece, pc_s.at[j], pc_r.at[j], inst=partner)

    def relay_core(j):
        px_c[j].wait_recv()
        piece = params.at[frm[j], :, theirs]
        pd_c[j] = send(piece, piece, pc_s.at[n + j], pc_r.at[n + j], inst=partner)

    relay(near[0])
    new_params(theirs)
    g_c.wait_recv()
    new_params(cols_of(partner))
    for j in near[1:]:
        relay(j)
    g_f.wait_recv()
    new_params(cols_of(diagonal))
    for j in near:
        relay_core(j)
    for j in near:
        pc_c[j].wait_recv()
        pd_c[j].wait_recv()
    for copy in nf_c:
        copy.wait_recv()
    for group in (core_c, x_c, z_c, pz_c, px_c, pc_c, pd_c):
        for copy in group.values():
            copy.wait_send()
    for copy in (nc, nx, g_x, g_c, g_f, *ny_c, *nz_c, *nf_c):
        copy.wait_send()


def local(
    n, tp,
    kernel_grads,
    kernel_master,
    kernel_first,
    kernel_second,
    gain_grads,
    gain_master,
    gain_first,
    gain_second,
):
    heads, depth, cols = kernel_grads.shape[1:]
    rows = depth // n
    norms = gain_grads.shape[1]
    half, quarter = cols // 2, cols // 4
    dma = pltpu.SemaphoreType.DMA
    vmem = pl.BlockSpec(memory_space=pltpu.VMEM)
    anyspace = pl.BlockSpec(memory_space=pl.ANY)
    params, gradient, gain_whole = pl.pallas_call(
        functools.partial(step_kernel, n, tp),
        out_shape=(
            jax.ShapeDtypeStruct((n, rows, cols), BF16),
            jax.ShapeDtypeStruct((rows, cols), BF16),
            jax.ShapeDtypeStruct((norms, cols), F32),
        ),
        in_specs=[anyspace] * 5,
        out_specs=(vmem, vmem, vmem),
        scratch_shapes=[
            pltpu.VMEM((n, rows, cols), BF16),
            pltpu.VMEM((n, rows, half), BF16),
            pltpu.VMEM((n, rows, quarter), BF16),
            pltpu.VMEM((n, rows, quarter), BF16),
            pltpu.VMEM((n, rows, quarter), BF16),
            pltpu.VMEM((n, rows, quarter), BF16),
            pltpu.VMEM((rows, cols), F32),
            pltpu.VMEM((rows, cols), F32),
            pltpu.VMEM((rows, cols), F32),
            pltpu.VMEM((norms, cols), BF16),
            pltpu.VMEM((norms, half), BF16),
            pltpu.VMEM((norms, quarter), BF16),
            pltpu.VMEM((norms, quarter), BF16),
            pltpu.VMEM((tp, norms, quarter), BF16),
            pltpu.VMEM((n, norms, quarter), BF16),
            dma((n + 4,)),
            dma((n,)), dma((n,)), dma((n,)), dma((n,)), dma((n,)), dma((n,)),
            dma((n,)), dma((n,)), dma((n,)), dma((n,)), dma((2 * n,)), dma((2 * n,)),
            dma((3,)), dma((3,)),
            dma((1,)), dma((1,)), dma((1,)), dma((1,)),
            dma((tp,)), dma((tp,)), dma((n,)), dma((n,)), dma((3,)), dma((3,)),
        ],
        compiler_params=pltpu.CompilerParams(collective_id=0, has_side_effects=True),
    )(
        kernel_grads.reshape(n, rows, cols),
        kernel_master.reshape(rows, cols),
        kernel_first.reshape(rows, cols),
        kernel_second.reshape(rows, cols),
        gain_grads.reshape(norms, cols),
    )
    kernel_params = params.reshape(heads, depth, cols)
    kernel_master_new, kernel_first_new, kernel_second_new = adam_update(
        gradient.astype(F32).reshape(kernel_master.shape),
        kernel_master, kernel_first, kernel_second,
    )
    gain_master_new, gain_first_new, gain_second_new = adam_update(
        gain_whole, gain_master, gain_first, gain_second
    )
    gain_params = gain_master_new.astype(BF16)
    return (
        kernel_params,
        kernel_master_new,
        kernel_first_new,
        kernel_second_new,
        gain_params,
        gain_master_new,
        gain_first_new,
        gain_second_new,
    )


def solution(mesh):
    return jax.shard_map(
        functools.partial(local, mesh.shape["dp"], mesh.shape["tp"]),
        mesh=mesh,
        in_specs=(
            P(("inst", "dp"), "tp", None, None),
            P("tp", "dp", None),
            P("tp", "dp", None),
            P("tp", "dp", None),
            P(("inst", "dp", "tp"), None, None),
            P(),
            P(),
            P(),
        ),
        out_specs=(
            P("tp", None, None),
            P("tp", "dp", None),
            P("tp", "dp", None),
            P("tp", "dp", None),
            P(),
            P(),
            P(),
            P(),
        ),
        check_vma=False,
    )
```

time: 143 us -> 39.9 us (0.28)
  waiting for transfers between devices: 68.4 us -> 0 us
  blocking collectives: 52.8 us -> 0 us
  Pallas kernels: 0 us -> 34.6 us
  between operations: 14.5 us -> 0.74 us
  local copies, waits for them, and re-layouts: 3.1 us -> 1.05 us
    pallas_call x0 -> x1, Pallas kernels: none -> 34.6 us  [local(): pl.pallas_call(functools.partial(step_kernel, n, tp), out_shape=(jax.Shap...]
    reduce_scatter x1 -> x0, waiting for transfers between devices: 34.4 us -> none  [local(): lax.psum_scatter(local_grads.astype(jnp.bfloat16), 'dp', scatter_dimensio...]
    psum x1 -> x0, waiting for transfers between devices: 33.3 us -> none  [local(): lax.psum(partial_rows.astype(jnp.bfloat16), 'inst').astype(jnp.float32)]
    unnamed x1 -> x0, blocking collectives: 20.5 us -> none
    psum x2 -> x0, blocking collectives: 19.1 us -> none  [the longest x1 10.9 us: local(): lax.psum(gain_piece.astype(jnp.bfloat16), 'inst').astype(jnp.float32)]
    all_gather x1 -> x0, blocking collectives: 13.2 us -> none  [local(): lax.all_gather(gain_piece, 'dp', axis=0, tiled=True)]
    convert_element_type x2 -> x1, other arithmetic: 3.55 us -> 0.8 us  [local(): gain_params = gain_master_new.astype(BF16)]
    sub x0 -> x1, other arithmetic: none -> 2.56 us  [adam_update(): master - learn_rate * (first_hat / (jnp.sqrt(second_hat) + epsilon) + dec...]
  transfers between devices with their start and end apart: 3 -> 0, of which waited for: 2 -> 0; matrix products, arithmetic and copies ran while one was open for 1% -> 0% of each run, Pallas kernels for 0% -> 0%
where the time goes in v1:
time: 39.9 us; the launch traced here: 39.8 us
  Pallas kernels  34.6 us (87%)
  other arithmetic  3.35 us (8%)
  local copies, waits for them, and re-layouts  1.05 us (3%)
  between operations  0.74 us (2%)
    pallas_call x1, Pallas kernels, local(): pl.pallas_call(functools.partial(step_kernel, n, tp), out_shape=(jax.Shap...  34.6 us
    sub x1, other arithmetic, adam_update(): master - learn_rate * (first_hat / (jnp.sqrt(second_hat) + epsilon) + dec...  2.56 us
    unnamed x17, local copies, waits for them, and re-layouts  1.05 us

profile of v1, /device:TPU:0, one launch (start us, length us, event | category | flops | bytes accessed | tf_op | source)
XLA Modules:
  0.0 39.8 jit_solution(10613491644551326575)
XLA Ops:
  0.6 0.0 copy-start
  0.6 0.0 copy-start.1
  0.7 0.0 copy-start.2
  0.7 34.6 %shard_map.143 = (bf16[4,32,4608]{2,1,0:T(8,128)(2,1)}, bf16[32,4608]{1,0:T(8,128)(2,1)}, f32[4,4608]{1,0:T(4,128)}) custom-call(bf16[4,32,4608]{2,1,0:T(8,128)(2,1)} %bitcast.19, f32[32,4608]{1,0:T(8,128)} %bitcast.16, f32[32,4608]{1,0:T(8,128)} %bitcast.17, f32[32,4608]{1,0:T(8,128)} %bitcast.18, bf16[4,4608]{1,0:T(4,128)(2,1)} %bitcast.21), custom_call_target="tpu_custom_call" | custom-call | tf_op jit(solution)/shard_map/pallas_call | solution.py:244
  35.3 0.0 copy-done
  35.3 0.0 copy-done.1
  35.3 0.0 copy-done.2
  35.3 0.0 copy-start.4
  35.3 0.0 copy-start.5
  35.3 0.0 copy-start.6
  35.4 0.0 copy-start.7
  35.4 0.0 copy-start.3
  35.4 2.6 %multiply_subtract_fusion = (f32[1,32,4608]{2,1,0:T(8,128)}, f32[1,32,4608]{2,1,0:T(8,128)}, f32[1,32,4608]{2,1,0:T(8,128)}) fusion(f32[1,32,4608]{2,1,0:T(8,128)S(1)} %copy-done, bf16[32,4608]{1,0:T(8,128)(2,1)} %get-tuple-element.12, f32[1,32,4608]{2,1,0:T(8,128)S(1)} %copy-done.1, f32[1,32,4608]{2,1,0:T(8,128)S(1)} %copy-done.2), kind=kLoop, calls=%fused_computation.6 | loop fusion | flops 2359296 | bytes 3833856 | tf_op jit(solution)/shard_map/sub | solution.py:26
  37.9 0.0 copy-done.4
  37.9 0.0 copy-done.5
  37.9 0.0 copy-done.6
  37.9 0.0 copy-done.7
  38.0 0.8 %fusion.5 = (bf16[4,4608]{1,0:T(4,128)(2,1)}, f32[4,4608]{1,0:T(4,128)}, f32[4,4608]{1,0:T(4,128)}, f32[4,4608]{1,0:T(4,128)}) fusion(f32[4,4608]{1,0:T(4,128)S(1)} %copy-done.4, f32[4,4608]{1,0:T(4,128)S(1)} %copy-done.7, f32[4,4608]{1,0:T(4,128)S(1)} %copy-done.5, f32[4,4608]{1,0:T(4,128)S(1)} %copy-done.6), kind=kLoop, calls=%fused_computation.11 | loop fusion | flops 294912 | bytes 552960 | tf_op jit(solution)/shard_map/convert_element_type | solution.py:292
  38.7 0.0 copy-done.3
  38.8 1.0 %copy.17 = bf16[1,128,4608]{2,1,0:T(8,128)(2,1)} copy(bf16[1,128,4608]{2,1,0:T(8,128)(2,1)S(1)} %bitcast.20) | data formatting | bytes 2359296
Async XLA Ops:
  0.6 34.7 %copy-start = (f32[1,32,4608]{2,1,0:T(8,128)S(1)}, f32[1,32,4608]{2,1,0:T(8,128)}, u32[]{:S(2)}) copy-start(f32[1,32,4608]{2,1,0:T(8,128)} %param.9) | copy-start | bytes 1769476
  0.6 34.7 %copy-start.1 = (f32[1,32,4608]{2,1,0:T(8,128)S(1)}, f32[1,32,4608]{2,1,0:T(8,128)}, u32[]{:S(2)}) copy-start(f32[1,32,4608]{2,1,0:T(8,128)} %param.10) | copy-start | bytes 1769476
  0.7 34.7 %copy-start.2 = (f32[1,32,4608]{2,1,0:T(8,128)S(1)}, f32[1,32,4608]{2,1,0:T(8,128)}, u32[]{:S(2)}) copy-start(f32[1,32,4608]{2,1,0:T(8,128)} %param.11) | copy-start | bytes 1769476
  35.3 2.6 %copy-start.4 = (f32[4,4608]{1,0:T(4,128)S(1)}, f32[4,4608]{1,0:T(4,128)}, u32[]{:S(2)}) copy-start(f32[4,4608]{1,0:T(4,128)} %param.13) | copy-start | bytes 221188
  35.3 2.6 %copy-start.5 = (f32[4,4608]{1,0:T(4,128)S(1)}, f32[4,4608]{1,0:T(4,128)}, u32[]{:S(2)}) copy-start(f32[4,4608]{1,0:T(4,128)} %param.14) | copy-start | bytes 221188
  35.3 2.6 %copy-start.6 = (f32[4,4608]{1,0:T(4,128)S(1)}, f32[4,4608]{1,0:T(4,128)}, u32[]{:S(2)}) copy-start(f32[4,4608]{1,0:T(4,128)} %param.15) | copy-start | bytes 221188
  35.4 2.6 %copy-start.7 = (f32[4,4608]{1,0:T(4,128)S(1)}, f32[4,4608]{1,0:T(4,128)}, u32[]{:S(2)}) copy-start(f32[4,4608]{1,0:T(4,128)} %get-tuple-element.13) | copy-start | bytes 221188
  35.4 3.4 %copy-start.3 = (bf16[4,32,4608]{2,1,0:T(8,128)(2,1)S(1)}, bf16[4,32,4608]{2,1,0:T(8,128)(2,1)}, u32[]{:S(2)}) copy-start(bf16[4,32,4608]{2,1,0:T(8,128)(2,1)} %get-tuple-element.11) | copy-start | bytes 3538948

commit v2 on v1

--- a/solution.py
+++ b/solution.py
@@ -47,8 +47,24 @@
     partner = me + 1 - 2 * core
     across = (me + 2) % 4
     diagonal = (partner + 2) % 4
-    order = sorted(range(1, n), key=lambda j: -min(j, n - j)) + [0]
-    near = sorted(range(1, n), key=lambda j: min(j, n - j))
+    rows = gv.shape[1]
+    parts = 2 if rows % 32 == 0 else 1
+    cut = rows // parts
+
+    def ranked(r):
+        low = jnp.minimum(z, n - 1 - z)
+        both = r <= 2 * low
+        dist = jnp.where(both, (r + 1) // 2, r - low)
+        up = jnp.where(both, 1 - r % 2, (2 * z < n - 1).astype(jnp.int32))
+        return z + (2 * up - 1) * dist
+
+    ring = {0: z, **{r: ranked(r) for r in range(1, n)}}
+    order = list(range(n - 1, -1, -1))
+    near = list(range(1, n))
+    pieces = [(r, p) for r in order for p in range(parts)]
+
+    def band(p):
+        return pl.ds(p * cut, cut)
 
     def span(start, size):
         return pl.ds(pl.multiple_of(start, 128), size)
@@ -69,9 +85,7 @@
         copy.start()
         return copy
 
-    to = {j: (z + j) % n for j in range(n)}
-    frm = {j: (z + n - j) % n for j in range(n)}
-    loads = {j: load(grads.at[to[j]], gv.at[to[j]], j) for j in order}
+    loads = {j: load(grads.at[ring[j]], gv.at[ring[j]], j) for j in order}
     load_gain = load(gains, nv, n)
     load_state = [
         load(a, b, n + 1 + k)
@@ -82,7 +96,7 @@
     for other in (partner, across, diagonal):
         pl.semaphore_signal(barrier, inc=1, device_id={"inst": other}, device_id_type=MESH)
     for j in range(1, n):
-        pl.semaphore_signal(barrier, inc=1, device_id={"dp": to[j]}, device_id_type=MESH)
+        pl.semaphore_signal(barrier, inc=1, device_id={"dp": ring[j]}, device_id_type=MESH)
     for j in range(1, tp):
         pl.semaphore_signal(
             barrier, inc=1, device_id={"tp": (y + j) % tp}, device_id_type=MESH
@@ -95,45 +109,51 @@
     sent = []
 
     core_c = {}
-    for j in order:
-        loads[j].wait()
-        core_c[j] = send(
-            gv.at[to[j], :, other_half], core_in.at[to[j]], core_s.at[j], core_r.at[j],
-            inst=partner,
+    for r, p in pieces:
+        if p == 0:
+            loads[r].wait()
+        k = ring[r]
+        core_c[r, p] = send(
+            gv.at[k, band(p), other_half], core_in.at[k, band(p)],
+            core_s.at[r, p], core_r.at[r, p], inst=partner,
         )
     load_gain.wait()
     nc = send(nv.at[:, other_half], nc_in, nc_s.at[0], nc_r.at[0], inst=partner)
 
     x_c = {}
-    for j in order:
-        core_c[j].wait_recv()
-        k = to[j]
-        x_out[k] = (
-            gv[k, :, theirs].astype(F32) + core_in[k, :, theirs_in].astype(F32)
+    for r, p in pieces:
+        core_c[r, p].wait_recv()
+        k, rows_p = ring[r], band(p)
+        x_out[k, rows_p] = (
+            gv[k, rows_p, theirs].astype(F32) + core_in[k, rows_p, theirs_in].astype(F32)
         ).astype(BF16)
-        x_c[j] = send(x_out.at[k], x_in.at[k], x_s.at[j], x_r.at[j], inst=across)
-        if j == order[0]:
+        x_c[r, p] = send(
+            x_out.at[k, rows_p], x_in.at[k, rows_p], x_s.at[r, p], x_r.at[r, p], inst=across
+        )
+        if (r, p) == pieces[1]:
             nc.wait_recv()
             nx_out[...] = (
                 nv[:, theirs].astype(F32) + nc_in[:, theirs_in].astype(F32)
             ).astype(BF16)
             nx = send(nx_out, nx_in, nx_s.at[0], nx_r.at[0], inst=across)
 
-    def chip_sum(k):
+    def chip_sum(k, rows_p):
         return (
-            gv[k, :, mine].astype(F32)
-            + core_in[k, :, mine_in].astype(F32)
-            + x_in[k].astype(F32)
+            gv[k, rows_p, mine].astype(F32)
+            + core_in[k, rows_p, mine_in].astype(F32)
+            + x_in[k, rows_p].astype(F32)
         )
 
     z_c = {}
     ny_c, nz_c = [], []
-    for j in order[:-1]:
-        x_c[j].wait_recv()
-        k = to[j]
-        z_out[j] = chip_sum(k).astype(BF16)
-        z_c[j] = send(z_out.at[j], z_in.at[j], z_s.at[j], z_r.at[j], dp=k)
-        if j == order[0]:
+    for r, p in pieces[: -parts]:
+        x_c[r, p].wait_recv()
+        k, rows_p = ring[r], band(p)
+        z_out[k, rows_p] = chip_sum(k, rows_p).astype(BF16)
+        z_c[r, p] = send(
+            z_out.at[k, rows_p], z_in.at[z, rows_p], z_s.at[r, p], z_r.at[z, p], dp=k
+        )
+        if (r, p) == pieces[1]:
             nx.wait_recv()
             ny[y] = (
                 nv[:, mine].astype(F32) + nc_in[:, mine_in].astype(F32)
@@ -149,31 +169,42 @@
     for i in range(1, tp):
         total += ny[i].astype(F32)
     nz[z] = total.astype(BF16)
-    for j in range(1, n):
-        nz_c.append(send(nz.at[z], nz.at[z], nz_s.at[j], nz_r.at[j], dp=to[j]))
-
-    x_c[0].wait_recv()
-    gradient = chip_sum(z)
+    for j in near:
+        nz_c.append(
+            send(nz.at[z], nz.at[z], nz_s.at[j], nz_r.at[j], dp=(z + j) % n)
+        )
+
+    def expect(ref, s, r, **where):
+        return pltpu.make_async_remote_copy(
+            src_ref=ref, dst_ref=ref, send_sem=s, recv_sem=r,
+            device_id=where, device_id_type=MESH,
+        )
+
     for copy in load_state:
         copy.wait()
-    for j in order[:-1]:
-        z_c[j].wait_recv()
-        gradient += z_in[j].astype(F32)
-    gsum[:, mine] = gradient.astype(BF16)
-
-    def new_params(where):
-        g = gsum[:, where].astype(F32)
-        fresh = adam_update(g, pv[:, where], mv[:, where], vv[:, where])[0]
-        params[z, :, where] = fresh.astype(BF16)
-
-    new_params(mine)
-    pz_c = {}
-    for j in near[::-1]:
-        pz_c[j] = send(
-            params.at[z, :, mine], params.at[z, :, mine], pz_s.at[j], pz_r.at[j], dp=to[j]
-        )
-    g_x = send(gsum.at[:, mine], gsum.at[:, mine], g_s.at[0], g_r.at[0], inst=across)
-    g_c = send(gsum.at[:, mine], gsum.at[:, mine], g_s.at[1], g_r.at[1], inst=partner)
+
+    def new_params(where, rows_p):
+        g = gsum[rows_p, where].astype(F32)
+        fresh = adam_update(g, pv[rows_p, where], mv[rows_p, where], vv[rows_p, where])[0]
+        params[z, rows_p, where] = fresh.astype(BF16)
+
+    pz_c, g_x, g_c, g_f = {}, {}, {}, {}
+    for p in range(parts):
+        rows_p = band(p)
+        x_c[0, p].wait_recv()
+        gradient = chip_sum(z, rows_p)
+        for r in near:
+            k = ring[r]
+            expect(z_in.at[k, rows_p], z_s.at[r, p], z_r.at[k, p], dp=k).wait_recv()
+            gradient += z_in[k, rows_p].astype(F32)
+        gsum[rows_p, mine] = gradient.astype(BF16)
+        new_params(mine, rows_p)
+        piece = params.at[z, rows_p, mine]
+        for r in near:
+            pz_c[r, p] = send(piece, piece, pz_s.at[r, p], pz_r.at[z, p], dp=ring[r])
+        piece = gsum.at[rows_p, mine]
+        g_x[p] = send(piece, piece, g_s.at[0, p], g_r.at[0, p], inst=across)
+        g_c[p] = send(piece, piece, g_s.at[1, p], g_r.at[1, p], inst=partner)
 
     for copy in nz_c:
         copy.wait_recv()
@@ -186,40 +217,51 @@
         for i, other in enumerate((partner, across, diagonal))
     ]
 
-    g_x.wait_recv()
-    g_f = send(gsum.at[:, theirs], gsum.at[:, theirs], g_s.at[2], g_r.at[2], inst=partner)
     px_c, pc_c, pd_c = {}, {}, {}
 
-    def relay(j):
-        pz_c[j].wait_recv()
-        piece = params.at[frm[j], :, mine]
-        px_c[j] = send(piece, piece, px_s.at[j], px_r.at[j], inst=across)
-        pc_c[j] = send(piece, piece, pc_s.at[j], pc_r.at[j], inst=partner)
-
-    def relay_core(j):
-        px_c[j].wait_recv()
-        piece = params.at[frm[j], :, theirs]
-        pd_c[j] = send(piece, piece, pc_s.at[n + j], pc_r.at[n + j], inst=partner)
+    def relay(r):
+        for p in range(parts):
+            k = ring[r]
+            piece = params.at[k, band(p), mine]
+            expect(piece, pz_s.at[r, p], pz_r.at[k, p], dp=k).wait_recv()
+            px_c[r, p] = send(piece, piece, px_s.at[r, p], px_r.at[r, p], inst=across)
+            pc_c[r, p] = send(piece, piece, pc_s.at[r, p], pc_r.at[r, p], inst=partner)
+
+    def relay_core(r):
+        for p in range(parts):
+            px_c[r, p].wait_recv()
+            piece = params.at[ring[r], band(p), theirs]
+            pd_c[r, p] = send(
+                piece, piece, pc_s.at[n + r, p], pc_r.at[n + r, p], inst=partner
+            )
 
     relay(near[0])
-    new_params(theirs)
-    g_c.wait_recv()
-    new_params(cols_of(partner))
-    for j in near[1:]:
-        relay(j)
-    g_f.wait_recv()
-    new_params(cols_of(diagonal))
-    for j in near:
-        relay_core(j)
-    for j in near:
-        pc_c[j].wait_recv()
-        pd_c[j].wait_recv()
+    for p in range(parts):
+        g_x[p].wait_recv()
+        piece = gsum.at[band(p), theirs]
+        g_f[p] = send(piece, piece, g_s.at[2, p], g_r.at[2, p], inst=partner)
+    for r in near[1:-1]:
+        relay(r)
+    for p in range(parts):
+        g_c[p].wait_recv()
+        new_params(theirs, band(p))
+        new_params(cols_of(partner), band(p))
+    for r in near[1:][-1:]:
+        relay(r)
+    for p in range(parts):
+        g_f[p].wait_recv()
+        new_params(cols_of(diagonal), band(p))
+    for r in near:
+        relay_core(r)
+    for key in pc_c:
+        pc_c[key].wait_recv()
+        pd_c[key].wait_recv()
     for copy in nf_c:
         copy.wait_recv()
-    for group in (core_c, x_c, z_c, pz_c, px_c, pc_c, pd_c):
+    for group in (core_c, x_c, z_c, pz_c, px_c, pc_c, pd_c, g_x, g_c, g_f):
         for copy in group.values():
             copy.wait_send()
-    for copy in (nc, nx, g_x, g_c, g_f, *ny_c, *nz_c, *nf_c):
+    for copy in (nc, nx, *ny_c, *nz_c, *nf_c):
         copy.wait_send()
 
 
@@ -238,9 +280,10 @@
     rows = depth // n
     norms = gain_grads.shape[1]
     half, quarter = cols // 2, cols // 4
+    parts = 2
     dma = pltpu.SemaphoreType.DMA
     vmem = pl.BlockSpec(memory_space=pltpu.VMEM)
-    anyspace = pl.BlockSpec(memory_space=pl.ANY)
+    hbm = pl.BlockSpec(memory_space=pltpu.HBM)
     params, gradient, gain_whole = pl.pallas_call(
         functools.partial(step_kernel, n, tp),
         out_shape=(
@@ -248,7 +291,7 @@
             jax.ShapeDtypeStruct((rows, cols), BF16),
             jax.ShapeDtypeStruct((norms, cols), F32),
         ),
-        in_specs=[anyspace] * 5,
+        in_specs=[hbm] * 5,
         out_specs=(vmem, vmem, vmem),
         scratch_shapes=[
             pltpu.VMEM((n, rows, cols), BF16),
@@ -267,19 +310,23 @@
             pltpu.VMEM((tp, norms, quarter), BF16),
             pltpu.VMEM((n, norms, quarter), BF16),
             dma((n + 4,)),
-            dma((n,)), dma((n,)), dma((n,)), dma((n,)), dma((n,)), dma((n,)),
-            dma((n,)), dma((n,)), dma((n,)), dma((n,)), dma((2 * n,)), dma((2 * n,)),
-            dma((3,)), dma((3,)),
+            *[dma((n, parts))] * 10,
+            dma((2 * n, parts)), dma((2 * n, parts)), dma((3, parts)), dma((3, parts)),
             dma((1,)), dma((1,)), dma((1,)), dma((1,)),
             dma((tp,)), dma((tp,)), dma((n,)), dma((n,)), dma((3,)), dma((3,)),
         ],
-        compiler_params=pltpu.CompilerParams(collective_id=0, has_side_effects=True),
+        compiler_params=pltpu.CompilerParams(collective_id=0, has_side_effects=True, vmem_limit_bytes=16 * 2**20),
     )(
-        kernel_grads.reshape(n, rows, cols),
-        kernel_master.reshape(rows, cols),
-        kernel_first.reshape(rows, cols),
-        kernel_second.reshape(rows, cols),
-        gain_grads.reshape(norms, cols),
+        *(
+            pltpu.with_memory_space_constraint(array, pltpu.HBM)
+            for array in (
+                kernel_grads.reshape(n, rows, cols),
+                kernel_master.reshape(rows, cols),
+                kernel_first.reshape(rows, cols),
+                kernel_second.reshape(rows, cols),
+                gain_grads.reshape(norms, cols),
+            )
+        )
     )
     kernel_params = params.reshape(heads, depth, cols)
     kernel_master_new, kernel_first_new, kernel_second_new = adam_update(

time: 39.9 us -> 34.9 us (0.87)
  Pallas kernels: 34.6 us -> 30.7 us
  other arithmetic: 3.35 us -> 2.31 us
    pallas_call x1, Pallas kernels: 34.6 us -> 30.7 us  [local(): pl.pallas_call(functools.partial(step_kernel, n, tp), out_shape=(jax.Shap...]
    sub x1, other arithmetic: 2.56 us -> 1.52 us  [adam_update(): master - learn_rate * (first_hat / (jnp.sqrt(second_hat) + epsilon) + dec...]
    unnamed x17 -> x13, local copies, waits for them, and re-layouts: 1.05 us -> 1.04 us
where the time goes in v2:
time: 34.9 us; the launch traced here: 34.8 us
  Pallas kernels  30.7 us (88%)
  other arithmetic  2.31 us (7%)
  local copies, waits for them, and re-layouts  1.04 us (3%)
  between operations  0.72 us (2%)
    pallas_call x1, Pallas kernels, local(): pl.pallas_call(functools.partial(step_kernel, n, tp), out_shape=(jax.Shap...  30.7 us
    sub x1, other arithmetic, adam_update(): master - learn_rate * (first_hat / (jnp.sqrt(second_hat) + epsilon) + dec...  1.52 us
    unnamed x13, local copies, waits for them, and re-layouts  1.04 us
    convert_element_type x1, other arithmetic, local(): gain_params = gain_master_new.astype(BF16)  0.8 us

profile of v2, /device:TPU:0, one launch (start us, length us, event | category | flops | bytes accessed | tf_op | source)
XLA Modules:
  0.0 34.8 jit_solution(17705503048999341113)
XLA Ops:
  0.6 0.0 copy-start
  0.6 0.0 copy-start.1
  0.7 0.0 copy-start.2
  0.7 30.7 %shard_map.143 = (bf16[4,32,4608]{2,1,0:T(8,128)(2,1)S(1)}, bf16[32,4608]{1,0:T(8,128)(2,1)S(1)}, f32[4,4608]{1,0:T(4,128)S(1)}) custom-call(bf16[4,32,4608]{2,1,0:T(8,128)(2,1)} %bitcast.20, f32[32,4608]{1,0:T(8,128)} %bitcast.17, f32[32,4608]{1,0:T(8,128)} %bitcast.18, f32[32,4608]{1,0:T(8,128)} %bitcast.19, bf16[4,4608]{1,0:T(4,128)(2,1)} %bitcast.21), custom_call_target="tpu_custom_call" | custom-call | tf_op jit(solution)/shard_map/pallas_call | solution.py:287
  31.4 0.0 copy-done
  31.4 0.0 copy-done.1
  31.4 0.0 copy-done.2
  31.4 0.0 copy-start.3
  31.4 0.0 copy-start.4
  31.4 0.0 copy-start.5
  31.5 1.5 %multiply_subtract_fusion = (f32[1,32,4608]{2,1,0:T(8,128)}, f32[1,32,4608]{2,1,0:T(8,128)}, f32[1,32,4608]{2,1,0:T(8,128)}) fusion(f32[1,32,4608]{2,1,0:T(8,128)S(1)} %copy-done, bf16[32,4608]{1,0:T(8,128)(2,1)S(1)} %get-tuple-element.12, f32[1,32,4608]{2,1,0:T(8,128)S(1)} %copy-done.1, f32[1,32,4608]{2,1,0:T(8,128)S(1)} %copy-done.2), kind=kLoop, calls=%fused_computation.6 | loop fusion | flops 2359296 | bytes 3833856 | tf_op jit(solution)/shard_map/sub | solution.py:26
  33.0 0.0 copy-done.3
  33.0 0.0 copy-done.4
  33.0 0.0 copy-done.5
  33.0 0.8 %fusion.5 = (bf16[4,4608]{1,0:T(4,128)(2,1)}, f32[4,4608]{1,0:T(4,128)}, f32[4,4608]{1,0:T(4,128)}, f32[4,4608]{1,0:T(4,128)}) fusion(f32[4,4608]{1,0:T(4,128)S(1)} %copy-done.3, f32[4,4608]{1,0:T(4,128)S(1)} %get-tuple-element.13, f32[4,4608]{1,0:T(4,128)S(1)} %copy-done.4, f32[4,4608]{1,0:T(4,128)S(1)} %copy-done.5), kind=kLoop, calls=%fused_computation.11 | loop fusion | flops 294912 | bytes 552960 | tf_op jit(solution)/shard_map/convert_element_type | solution.py:339
  33.8 1.0 %copy.17 = bf16[1,128,4608]{2,1,0:T(8,128)(2,1)} copy(bf16[1,128,4608]{2,1,0:T(8,128)(2,1)S(1)} %bitcast.16) | data formatting | bytes 2359296
Async XLA Ops:
  0.6 30.8 %copy-start = (f32[1,32,4608]{2,1,0:T(8,128)S(1)}, f32[1,32,4608]{2,1,0:T(8,128)}, u32[]{:S(2)}) copy-start(f32[1,32,4608]{2,1,0:T(8,128)} %param.9) | copy-start | bytes 1769476
  0.6 30.8 %copy-start.1 = (f32[1,32,4608]{2,1,0:T(8,128)S(1)}, f32[1,32,4608]{2,1,0:T(8,128)}, u32[]{:S(2)}) copy-start(f32[1,32,4608]{2,1,0:T(8,128)} %param.10) | copy-start | bytes 1769476
  0.7 30.8 %copy-start.2 = (f32[1,32,4608]{2,1,0:T(8,128)S(1)}, f32[1,32,4608]{2,1,0:T(8,128)}, u32[]{:S(2)}) copy-start(f32[1,32,4608]{2,1,0:T(8,128)} %param.11) | copy-start | bytes 1769476
  31.4 1.6 %copy-start.3 = (f32[4,4608]{1,0:T(4,128)S(1)}, f32[4,4608]{1,0:T(4,128)}, u32[]{:S(2)}) copy-start(f32[4,4608]{1,0:T(4,128)} %param.13) | copy-start | bytes 221188
  31.4 1.5 %copy-start.4 = (f32[4,4608]{1,0:T(4,128)S(1)}, f32[4,4608]{1,0:T(4,128)}, u32[]{:S(2)}) copy-start(f32[4,4608]{1,0:T(4,128)} %param.14) | copy-start | bytes 221188
  31.4 1.5 %copy-start.5 = (f32[4,4608]{1,0:T(4,128)S(1)}, f32[4,4608]{1,0:T(4,128)}, u32[]{:S(2)}) copy-start(f32[4,4608]{1,0:T(4,128)} %param.15) | copy-start | bytes 221188
